TPU v7x, 32 devices: a whole 2x2x4 slice. The times are simulated.
32 devices in a mesh: tm: 8 (over z, y), chan: 4 (over x, core).
Axes of the slice: x: 2, y: 2, z: 4, core: 2. Of those that a mesh axis runs over, the one named last changes fastest.
Arguments:
- series: float32 [256, 2048], P('chan', 'tm'), may hold values from -6 to 6
- lengths: int32 [16], replicated, may hold values from 42 to 128
Outputs:
- peak: float32 [2048], P('tm')
All inputs are finite; a program needn't handle non-finite values.
Results may differ from a plain program's by a relative error of at most 0.0015.
Values may be sent and summed in bfloat16 or wider, within the bound.
A program may use at most 128 MiB of HBM per device.

v0:
```python
import jax
import jax.numpy as jnp
from jax import lax
from jax.sharding import PartitionSpec as P

WIN = 256
STEPS = 2


EPS = 1e-05
MASKED = -1000000000.0


def passed_along(block, axis, distance):
    devices = range(lax.axis_size(axis))
    route = [(i - distance, i) for i in devices if i - distance in devices]
    return lax.ppermute(block, axis, route)


def windows_of(extended):
    count = extended.shape[1] - WIN + 1
    zeros = jnp.zeros((extended.shape[0], 1), jnp.float32)
    running = jnp.cumsum(jnp.concatenate([zeros, extended], axis=1), axis=1)
    running_sq = jnp.cumsum(jnp.concatenate([zeros, extended * extended], axis=1), axis=1)
    mean_val = (running[:, WIN:] - running[:, :count]) * (1.0 / WIN)
    mean_sq = (running_sq[:, WIN:] - running_sq[:, :count]) * (1.0 / WIN)
    spread = jnp.maximum(mean_sq - mean_val * mean_val, 0.0)
    scale = lax.rsqrt(spread + EPS)
    starts = jnp.arange(count, dtype=jnp.int32)
    index = starts[:, None] + jnp.arange(WIN, dtype=jnp.int32)[None, :]
    gathered = extended[:, index]
    normed = (gathered - mean_val[:, :, None]) * scale[:, :, None]
    return normed.astype(jnp.bfloat16)


def validity(block, lengths, rows, total):
    local = jnp.arange(rows, dtype=jnp.int32)
    seg_len = rows // 2
    pair = lax.dynamic_slice_in_dim(lengths, block * 2, 2)
    limit = jnp.where(local < seg_len, pair[0], pair[1])
    offset = local % seg_len
    return (offset < limit) & (block * rows + local <= total - WIN)


def body(series, lengths):
    rows = series.shape[1]
    total = rows * lax.axis_size("tm")
    excl = WIN // 4
    block = lax.axis_index("tm")
    tail = passed_along(series[:, : WIN - 1], "tm", -1)
    extended = jnp.concatenate([series, tail], axis=1)
    rows_z = windows_of(extended)
    rows_ok = validity(block, lengths, rows, total)
    local = jnp.arange(rows, dtype=jnp.int32)
    best = jnp.full((local.shape[0],), MASKED, jnp.float32)
    cols_z = rows_z
    for step in range(STEPS + 1):
        if step > 0:
            cols_z = passed_along(cols_z, "tm", 1)
        other = block - step
        safe = jnp.maximum(other, 0)
        cols_ok = validity(safe, lengths, rows, total) & (other >= 0)
        partial_value = lax.dot_general(
            rows_z, cols_z, (((0, 2), (0, 2)), ((), ())), preferred_element_type=jnp.float32
        )
        summed = lax.psum(partial_value, "chan")
        score = summed * (1.0 / WIN)
        lag = step * rows + local[:, None] - local[None, :]
        keep = rows_ok[:, None] & cols_ok[None, :] & (lag >= excl)
        best = jnp.maximum(best, jnp.max(jnp.where(keep, score, MASKED), axis=1))
    peak = jnp.where(best > 0.5 * MASKED, best, 0.0)
    return peak


def solution(mesh):
    return jax.shard_map(
        body,
        mesh=mesh,
        in_specs=(P("chan", "tm"), P()),
        out_specs=P("tm"),
        check_vma=False,
    )
```

profile of v0, /device:TPU:0, one launch (start us, length us, event | category | flops | bytes accessed | tf_op | source)
XLA Modules:
  0.0 691.5 jit_solution(8376566637861417019)
XLA Ops:
  6.5 0.9 copy.10
  7.5 1.3 collective-permute-start
  9.0 6.9 collective-permute-done
  16.1 1.2 reduce-window.16
  17.6 0.9 copy_bitcast_fusion.2
  18.5 1.2 reduce-window.14
  20.0 215.5 %gather_fusion = f32[65536,64]{1,0:T(8,128)} fusion(f32[64,511]{0,1:T(8,128)S(1)} %get-tuple-element.14, s32[65536]{0:T(1024)S(1)} %broadcast_clamp_fusion), kind=kCustom, calls=%fused_computation | custom fusion | bytes 33816576 | tf_op jit(solution)/shard_map/gather | solution.py:31
  235.5 26.2 %copy.17 = f32[256,256,64]{1,0,2:T(8,128)} copy(f32[256,256,64]{2,1,0:T(8,128)} %bitcast.49) | data formatting | bytes 33554432 | tf_op jit(solution)/shard_map/gather | solution.py:31
  261.8 7.6 %fusion.1 = bf16[64,256,256]{2,1,0:T(8,128)(2,1)S(1)} fusion(f32[256,256,64]{1,0,2:T(8,128)} %copy.17, f32[64,256]{1,0:T(8,128)S(1)} %get-tuple-element.11, f32[64,256]{1,0:T(8,128)S(1)} %get-tuple-element.12), kind=kLoop, calls=%fused_computation.3 | loop fusion | flops 12582912 | bytes 25296896 | tf_op jit(solution)/shard_map/convert_element_type | solution.py:33
  269.5 3.2 copy-done
  272.7 7.7 %collective-permute-start.1 = (bf16[64,256,256]{2,1,0:T(8,128)(2,1)S(1)}, bf16[64,256,256]{2,1,0:T(8,128)(2,1)}, u32[]{:S(2)}, u32[]{:S(2)}) collective-permute-start(bf16[64,256,256]{2,1,0:T(8,128)(2,1)S(1)} %fusion.1), channel_id=1, source_target_pairs={{0,4},{4,8},{8,12},{12,16},{16,20},{20,24},{24,28},{1,5},{5,9},{9,... | collective-permute-start | bytes 25165832 | tf_op jit(solution)/shard_map/ppermute | solution.py:17
  280.4 175.6 %collective-permute-done.1 = bf16[64,256,256]{2,1,0:T(8,128)(2,1)} collective-permute-done((bf16[64,256,256]{2,1,0:T(8,128)(2,1)S(1)}, bf16[64,256,256]{2,1,0:T(8,128)(2,1)}, u32[]{:S(2)}, u32[]{:S(2)}) %collective-permute-start.1) | collective-permute-done | bytes 8388640 | tf_op jit(solution)/shard_map/ppermute | solution.py:17
  456.1 7.7 %collective-permute-start.2 = (bf16[64,256,256]{2,1,0:T(8,128)(2,1)}, bf16[64,256,256]{2,1,0:T(8,128)(2,1)}, u32[]{:S(2)}, u32[]{:S(2)}) collective-permute-start(bf16[64,256,256]{2,1,0:T(8,128)(2,1)} %collective-permute-done.1), channel_id=1, source_target_pairs={{0,4},{4,8},{8,12},{12,16},{16,20},{20,24},{24,28},{1,5},{5,9},{9,... | collective-permute-start | bytes 25165832 | tf_op jit(solution)/shard_map/ppermute | solution.py:17
  463.8 0.6 fusion.17
  464.4 1.3 compare_and_fusion
  466.3 9.0 %convolution_bitcast_fusion.2 = f32[256,256]{1,0:T(8,128)} fusion(bf16[64,256,256]{2,1,0:T(8,128)(2,1)} %copy-done), kind=kOutput, calls=%fused_computation.6 | convolution fusion | flops 2147483648 | bytes 8650752 | tf_op jit(solution)/shard_map/dot_general | solution.py:63
  475.3 6.4 convolution_bitcast_fusion.1
  481.7 157.1 %collective-permute-done.2 = bf16[64,256,256]{2,1,0:T(8,128)(2,1)} collective-permute-done((bf16[64,256,256]{2,1,0:T(8,128)(2,1)}, bf16[64,256,256]{2,1,0:T(8,128)(2,1)}, u32[]{:S(2)}, u32[]{:S(2)}) %collective-permute-start.2) | collective-permute-done | bytes 8388640 | tf_op jit(solution)/shard_map/ppermute | solution.py:17
  638.8 6.4 convolution_bitcast_fusion
  645.3 1.2 and_and_fusion
  646.5 1.2 and_and_fusion.1
  647.8 1.2 and_and_fusion.2
  649.0 33.6 %all-reduce.4.cloned.1.call-done = (f32[256,256]{1,0:T(8,128)}, f32[256,256]{1,0:T(8,128)}, f32[256,256]{1,0:T(8,128)}) async-done(((f32[256,256]{1,0:T(8,128)}, f32[256,256]{1,0:T(8,128)}, f32[256,256]{1,0:T(8,128)}), (f32[256,256]{1,0:T(8,128)}, f32[256,256]{1,0:T(8,128)}, f32[256,256]{1,0:T(8,128)})) %all-reduce.4.cloned.1.call-update) | async-done | bytes 786448 | tf_op jit(solution)/shard_map/psum | solution.py:66
  682.6 1.5 select_reduce_fusion.2
  (33 shorter events, 2.4 us)
Async XLA Ops:
  6.5 676.0 %all-reduce.4.cloned.1.call-start = ((), (), s32[]{:S(2)}) async-start(), calls=%async_computation | async-start | bytes 1572864 | tf_op jit(solution)/shard_map/psum | solution.py:66
  7.5 8.4 %collective-permute-start = (f32[64,255]{0,1:T(8,128)S(1)}, f32[64,255]{0,1:T(8,128)S(1)}, u32[]{:S(2)}, u32[]{:S(2)}) collective-permute-start(f32[64,255]{0,1:T(8,128)S(1)} %bitcast.52), channel_id=1, source_target_pairs={{4,0},{8,4},{12,8},{16,12},{20,16},{24,20},{28,24},{5,1},{9,5},{13... | collective-permute-start | bytes 195848 | tf_op jit(solution)/shard_map/ppermute | solution.py:17
  17.5 218.0 %copy-start.3 = (f32[64,5]{0,1:T(8,128)}, f32[64,5]{0,1:T(8,128)S(1)}, u32[]{:S(2)}) copy-start(f32[64,5]{0,1:T(8,128)S(1)} %reduce-window.19) | copy-start | bytes 3844
  20.0 215.5 %copy-start.2 = (f32[64,5]{0,1:T(8,128)}, f32[64,5]{0,1:T(8,128)S(1)}, u32[]{:S(2)}) copy-start(f32[64,5]{0,1:T(8,128)S(1)} %reduce-window.15) | copy-start | bytes 3844
  235.5 26.2 %slice-start = ((f32[64,5]{0,1:T(8,128)}), f32[64,4]{0,1:T(4,128)S(1)}, s32[]{:S(2)}) async-start(f32[64,5]{0,1:T(8,128)} %copy-done.2), calls=%async_computation.1 | async-start | bytes 4096 | tf_op jit(solution)/shard_map/slice.1
  235.5 26.2 %slice-start.1 = ((f32[64,5]{0,1:T(8,128)}), f32[64,4]{0,1:T(4,128)S(1)}, s32[]{:S(2)}) async-start(f32[64,5]{0,1:T(8,128)} %copy-done.3), calls=%async_computation.2 | async-start | bytes 4096 | tf_op jit(solution)/shard_map/slice.3
  261.8 201.9 %copy-start.4 = (s32[16]{0:T(128)S(1)}, s32[16]{0:T(128)}, u32[]{:S(2)}) copy-start(s32[16]{0:T(128)} %param.3) | copy-start | bytes 196
  269.5 3.2 copy-start
  272.7 183.4 %collective-permute-start.1 = (bf16[64,256,256]{2,1,0:T(8,128)(2,1)S(1)}, bf16[64,256,256]{2,1,0:T(8,128)(2,1)}, u32[]{:S(2)}, u32[]{:S(2)}) collective-permute-start(bf16[64,256,256]{2,1,0:T(8,128)(2,1)S(1)} %fusion.1), channel_id=1, source_target_pairs={{0,4},{4,8},{8,12},{12,16},{16,20},{20,24},{24,28},{1,5},{5,9},{9,... | collective-permute-start | bytes 25165832 | tf_op jit(solution)/shard_map/ppermute | solution.py:17
  456.1 182.8 %collective-permute-start.2 = (bf16[64,256,256]{2,1,0:T(8,128)(2,1)}, bf16[64,256,256]{2,1,0:T(8,128)(2,1)}, u32[]{:S(2)}, u32[]{:S(2)}) collective-permute-start(bf16[64,256,256]{2,1,0:T(8,128)(2,1)} %collective-permute-done.1), channel_id=1, source_target_pairs={{0,4},{4,8},{8,12},{12,16},{16,20},{20,24},{24,28},{1,5},{5,9},{9,... | collective-permute-start | bytes 25165832 | tf_op jit(solution)/shard_map/ppermute | solution.py:17
  466.3 9.0 %copy-start.1 = (bf16[64,256,256]{2,1,0:T(8,128)(2,1)S(1)}, bf16[64,256,256]{2,1,0:T(8,128)(2,1)}, u32[]{:S(2)}) copy-start(bf16[64,256,256]{2,1,0:T(8,128)(2,1)} %copy-done) | copy-start | bytes 25165828
Sparse Core Ops, SparseCore 0:
  645.4 37.0 all-reduce.3
where the time goes:
time: 692 us; the launch traced here: 691 us
  waiting for transfers between devices  373 us (54%)
  local copies, waits for them, and re-layouts  248 us (36%)
  matrix products  21.9 us (3%)
  other arithmetic  18.3 us (3%)
  starting transfers between devices  16.7 us (2%)
  between operations  13.6 us (2%)
    ppermute x3, waiting for transfers between devices, passed_along(): return lax.ppermute(block, axis, route)  340 us
    gather x2, local copies, waits for them, and re-layouts, windows_of(): gathered = extended[:, index]  242 us
    psum x1, waiting for transfers between devices, body(): summed = lax.psum(partial_value, 'chan')  33.6 us
    dot_general x3, matrix products, body(): lax.dot_general(rows_z, cols_z, (((0, 2), (0, 2)), ((), ())), preferred_e...  21.9 us
    ppermute x3, starting transfers between devices, passed_along(): return lax.ppermute(block, axis, route)  16.7 us
  transfers between devices with their start and end apart: 4, of which 4 were waited for; matrix products, arithmetic and copies ran while one was open for 3% of the time, Pallas kernels for 0%

commit v1 on v0

v1 whole, which is shorter than its diff:
```python
import functools

import jax
import jax.numpy as jnp
from jax import lax
from jax.experimental import pallas as pl
from jax.experimental.pallas import tpu as pltpu
from jax.sharding import PartitionSpec as P

WIN = 256
STEPS = 2
GROUP = 8
EPS = 1e-05
MASKED = -1000000000.0
MESH = pl.DeviceIdType.MESH


def window_stats(x):
    width = x.shape[1]
    mean, second = x, None
    span = 1
    while span < WIN:
        later = pltpu.roll(mean, width - span, 1)
        gap = later - mean
        added = gap * gap * (span * 0.5)
        second = added if second is None else second + pltpu.roll(second, width - span, 1) + added
        mean = (mean + later) * 0.5
        span *= 2
    return mean, lax.rsqrt(second * (1.0 / WIN) + EPS)


def kernel(n_tm, n_chan, lengths, series, out, halo, xw, mu, sc, zown, zbuf, acc, recvbuf, peaks,
           halo_send, halo_recv, part_send, part_recv, peak_send, peak_recv):
    depth, rows = series.shape
    own = rows // n_chan
    total = rows * n_tm
    excl = WIN // 4
    block = lax.axis_index("tm")
    part = lax.axis_index("chan")

    def at(distance):
        return lax.rem(block + distance + n_tm, n_tm)

    def peer(d):
        return lax.rem(part + d, n_chan)

    barrier = pltpu.get_barrier_semaphore()
    greet = [(at(d), part) for d in (1, -1, -2)] + [(block, peer(d)) for d in range(1, n_chan)]
    for target in greet:
        pl.semaphore_signal(barrier, inc=1, device_id=target, device_id_type=MESH)
    pl.semaphore_wait(barrier, len(greet))

    halo_copies = []
    for slot, distance in enumerate((-1, 1, 2)):
        copy = pltpu.make_async_remote_copy(
            src_ref=series, dst_ref=halo.at[slot], send_sem=halo_send.at[slot], recv_sem=halo_recv.at[slot],
            device_id=(at(distance), part), device_id_type=MESH)
        copy.start()
        halo_copies.append(copy)

    def build_channel(r, x8, mu8, sc8, store):
        width = x8.shape[1]
        row = jnp.broadcast_to(x8[r:r + 1, :], (16, width))
        spread = pltpu.roll(row, width - 15, 1, stride=1, stride_axis=0)
        m = jnp.broadcast_to(mu8[r:r + 1, :], (16, rows))
        s = jnp.broadcast_to(sc8[r:r + 1, :], (16, rows))
        for q in range(8):
            moved = spread if q == 0 else pltpu.roll(spread, width - 16 * q, 1)
            for half in range(WIN // 128):
                z = (moved[:, 128 * half:128 * half + rows] - m) * s
                store(128 * half + 16 * q, z.astype(jnp.bfloat16))

    def stage(step):
        if step == 0:
            halo_copies[0].wait_recv()
            after = jnp.where(block == n_tm - 1, 0.0, halo[0])
            here = series[...]
        else:
            halo_copies[step].wait_recv()
            here = halo[step]
            after = series[...] if step == 1 else halo[1]
        x = jnp.concatenate([here, after], axis=1)
        xw[...] = x
        mean, scale = window_stats(x)
        mu[...] = mean[:, :rows]
        sc[...] = scale[:, :rows]

        acc[step] = jnp.zeros((rows, rows), jnp.float32)

        def group(g, carry):
            rows8 = pl.ds(pl.multiple_of(g * GROUP, GROUP), GROUP)
            x8, mu8, sc8 = xw[rows8, :], mu[rows8, :], sc[rows8, :]
            for r in range(GROUP):
                def store(k, value, r=r):
                    zbuf[r * WIN + k:r * WIN + k + 16, :] = value
                build_channel(r, x8, mu8, sc8, store)
            if step == 0:
                zown[g] = zbuf[...].T
            acc[step] += jnp.dot(zown[g], zbuf[...], preferred_element_type=jnp.float32)
            return carry

        lax.fori_loop(0, depth // GROUP, group, 0)

        copies = []
        for d in range(1, n_chan):
            copy = pltpu.make_async_remote_copy(
                src_ref=acc.at[step, pl.ds(pl.multiple_of(peer(d) * own, own), own), :],
                dst_ref=recvbuf.at[step, d - 1],
                send_sem=part_send.at[step, d - 1], recv_sem=part_recv.at[step, d - 1],
                device_id=(block, peer(d)), device_id_type=MESH)
            copy.start()
            copies.append(copy)
        return copies

    sent = [stage(step) for step in range(STEPS + 1)]

    seg_len = rows // 2
    row_at = part * own + lax.broadcasted_iota(jnp.int32, (own, rows), 0)
    col_at = lax.broadcasted_iota(jnp.int32, (own, rows), 1)

    def valid(which, local):
        limit = jnp.where(local < seg_len, lengths[which * 2], lengths[which * 2 + 1])
        offset = jnp.where(local < seg_len, local, local - seg_len)
        return (offset < limit) & (which * rows + local <= total - WIN)

    rows_ok = valid(block, row_at)
    best = jnp.full((own, rows), MASKED, jnp.float32)
    for step in range(STEPS + 1):
        other = block - step
        safe = jnp.maximum(other, 0)
        keep = rows_ok & valid(safe, col_at) & (other >= 0) & (step * rows + row_at - col_at >= excl)
        summed = acc[step, pl.ds(pl.multiple_of(part * own, own), own), :]
        for d in range(1, n_chan):
            sent[step][d - 1].wait_recv()
            summed = summed + recvbuf[step, d - 1]
        best = jnp.maximum(best, jnp.where(keep, summed * (1.0 / WIN), MASKED))
    folded = best[:, :128]
    for at_lane in range(128, rows, 128):
        folded = jnp.maximum(folded, best[:, at_lane:at_lane + 128])
    top = jnp.max(folded.T, axis=0, keepdims=True)
    top = jnp.where(top > 0.5 * MASKED, top, 0.0)
    padded = jnp.concatenate([top, jnp.zeros((1, 128 - own), jnp.float32)], axis=1)
    peaks[0] = jnp.broadcast_to(padded, (8, 128))
    copies = []
    for d in range(1, n_chan):
        copy = pltpu.make_async_remote_copy(
            src_ref=peaks.at[0], dst_ref=peaks.at[d],
            send_sem=peak_send.at[d - 1], recv_sem=peak_recv.at[d - 1],
            device_id=(block, peer(d)), device_id_type=MESH)
        copy.start()
        copies.append(copy)
    for copy in copies:
        copy.wait_recv()
    slots = [peaks[d, 0:1, :own] for d in range(n_chan)]
    pieces = []
    for q in range(n_chan):
        piece = slots[0]
        for d in range(1, n_chan):
            piece = jnp.where(lax.rem(part + n_chan - d, n_chan) == q, slots[d], piece)
        pieces.append(piece)
    out[...] = jnp.concatenate(pieces, axis=1)

    for copy in halo_copies + [c for step in sent for c in step] + copies:
        copy.wait_send()


def solution(mesh):
    n_tm, n_chan = mesh.shape["tm"], mesh.shape["chan"]

    def body(series, lengths):
        depth, rows = series.shape
        own = rows // n_chan
        vmem = pl.BlockSpec(memory_space=pltpu.VMEM)
        peak = pl.pallas_call(
            functools.partial(kernel, n_tm, n_chan),
            out_shape=jax.ShapeDtypeStruct((1, rows), jnp.float32),
            in_specs=[pl.BlockSpec(memory_space=pltpu.SMEM), vmem],
            out_specs=vmem,
            scratch_shapes=[
                pltpu.VMEM((STEPS + 1, depth, rows), jnp.float32),
                pltpu.VMEM((depth, 2 * rows), jnp.float32),
                pltpu.VMEM((depth, rows), jnp.float32),
                pltpu.VMEM((depth, rows), jnp.float32),
                pltpu.VMEM((depth // GROUP, rows, GROUP * WIN), jnp.bfloat16),
                pltpu.VMEM((GROUP * WIN, rows), jnp.bfloat16),
                pltpu.VMEM((STEPS + 1, rows, rows), jnp.float32),
                pltpu.VMEM((STEPS + 1, n_chan - 1, own, rows), jnp.float32),
                pltpu.VMEM((n_chan, 8, 128), jnp.float32),
                pltpu.SemaphoreType.DMA((STEPS + 1,)),
                pltpu.SemaphoreType.DMA((STEPS + 1,)),
                pltpu.SemaphoreType.DMA((STEPS + 1, n_chan - 1)),
                pltpu.SemaphoreType.DMA((STEPS + 1, n_chan - 1)),
                pltpu.SemaphoreType.DMA((n_chan - 1,)),
                pltpu.SemaphoreType.DMA((n_chan - 1,)),
            ],
            compiler_params=pltpu.CompilerParams(collective_id=0, has_side_effects=True),
        )(lengths, series)
        return peak.reshape(rows)

    return jax.shard_map(
        body, mesh=mesh, in_specs=(P("chan", "tm"), P()), out_specs=P("tm"), check_vma=False)
```

time: 692 us -> 50.5 us (0.07)
  waiting for transfers between devices: 373 us -> 0 us
  local copies, waits for them, and re-layouts: 248 us -> 1.22 us
  Pallas kernels: 0 us -> 48.5 us
  matrix products: 21.9 us -> 0 us
  other arithmetic: 18.3 us -> 0 us
  starting transfers between devices: 16.7 us -> 0 us
  between operations: 13.6 us -> 0.02 us
    ppermute x3 -> x0, waiting for transfers between devices: 340 us -> none  [passed_along(): return lax.ppermute(block, axis, route)]
    gather x2 -> x0, local copies, waits for them, and re-layouts: 242 us -> none  [windows_of(): gathered = extended[:, index]]
    pallas_call x0 -> x1, Pallas kernels: none -> 48.5 us  [body(): pl.pallas_call(functools.partial(kernel, n_tm, n_chan), out_shape=jax.Sha...]
    psum x1 -> x0, waiting for transfers between devices: 33.6 us -> none  [body(): summed = lax.psum(partial_value, 'chan')]
    dot_general x3 -> x0, matrix products: 21.9 us -> none  [body(): lax.dot_general(rows_z, cols_z, (((0, 2), (0, 2)), ((), ())), preferred_e...]
    ppermute x3 -> x0, starting transfers between devices: 16.7 us -> none  [passed_along(): return lax.ppermute(block, axis, route)]
    convert_element_type x1 -> x0, other arithmetic: 7.6 us -> none  [windows_of(): return normed.astype(jnp.bfloat16)]
  transfers between devices with their start and end apart: 4 -> 0, of which waited for: 4 -> 0; matrix products, arithmetic and copies ran while one was open for 3% -> 0% of each run, Pallas kernels for 0% -> 0%
where the time goes in v1:
time: 50.5 us; the launch traced here: 49.8 us
  Pallas kernels  48.5 us (96%)
  local copies, waits for them, and re-layouts  1.22 us (2%)
    pallas_call x1, Pallas kernels, body(): pl.pallas_call(functools.partial(kernel, n_tm, n_chan), out_shape=jax.Sha...  48.5 us
    unnamed x3, local copies, waits for them, and re-layouts  1.22 us

profile of v1, /device:TPU:0, one launch (start us, length us, event | category | flops | bytes accessed | tf_op | source)
XLA Modules:
  0.0 49.8 jit_solution(17651311703251516692)
XLA Ops:
  0.0 48.5 %shard_map.28 = f32[1,256]{1,0:T(1,128)} custom-call(s32[16]{0:T(128)} %lengths.1, f32[64,256]{1,0:T(8,128)} %series.1), custom_call_target="tpu_custom_call" | custom-call | tf_op jit(solution)/shard_map/pallas_call | solution.py:174
  48.5 0.0 copy-start
  48.5 0.7 %copy-done = f32[1,256]{1,0:T(1,128)S(1)} copy-done((f32[1,256]{1,0:T(1,128)S(1)}, f32[1,256]{1,0:T(1,128)}, u32[]{:S(2)}) %copy-start) | copy-done | bytes 1048
  49.2 0.6 %copy.4 = f32[256]{0:T(256)} copy(f32[256]{0:T(256)S(1)} %bitcast.1) | data formatting | bytes 2048
Async XLA Ops:
  48.5 0.7 %copy-start = (f32[1,256]{1,0:T(1,128)S(1)}, f32[1,256]{1,0:T(1,128)}, u32[]{:S(2)}) copy-start(f32[1,256]{1,0:T(1,128)} %shard_map.28) | copy-start | bytes 3076

commit v2 on v1

--- a/solution.py
+++ b/solution.py
@@ -9,27 +9,13 @@
 
 WIN = 256
 STEPS = 2
-GROUP = 8
+GROUP = 16
 EPS = 1e-05
 MASKED = -1000000000.0
 MESH = pl.DeviceIdType.MESH
 
 
-def window_stats(x):
-    width = x.shape[1]
-    mean, second = x, None
-    span = 1
-    while span < WIN:
-        later = pltpu.roll(mean, width - span, 1)
-        gap = later - mean
-        added = gap * gap * (span * 0.5)
-        second = added if second is None else second + pltpu.roll(second, width - span, 1) + added
-        mean = (mean + later) * 0.5
-        span *= 2
-    return mean, lax.rsqrt(second * (1.0 / WIN) + EPS)
-
-
-def kernel(n_tm, n_chan, lengths, series, out, halo, xw, mu, sc, zown, zbuf, acc, recvbuf, peaks,
+def kernel(n_tm, n_chan, lengths, series, out, halo, xt, moments, mu, sc, z0, z1, z2, acc, recvbuf, peaks,
            halo_send, halo_recv, part_send, part_recv, peak_send, peak_recv):
     depth, rows = series.shape
     own = rows // n_chan
@@ -58,49 +44,51 @@
         copy.start()
         halo_copies.append(copy)
 
-    def build_channel(r, x8, mu8, sc8, store):
-        width = x8.shape[1]
-        row = jnp.broadcast_to(x8[r:r + 1, :], (16, width))
-        spread = pltpu.roll(row, width - 15, 1, stride=1, stride_axis=0)
-        m = jnp.broadcast_to(mu8[r:r + 1, :], (16, rows))
-        s = jnp.broadcast_to(sc8[r:r + 1, :], (16, rows))
-        for q in range(8):
-            moved = spread if q == 0 else pltpu.roll(spread, width - 16 * q, 1)
-            for half in range(WIN // 128):
-                z = (moved[:, 128 * half:128 * half + rows] - m) * s
-                store(128 * half + 16 * q, z.astype(jnp.bfloat16))
-
-    def stage(step):
+    half = WIN // 2
+    reach = rows + half
+    chunks = half // GROUP
+    windows = (z0, z1, z2)
+
+    def prepare(step):
+        halo_copies[step].wait_recv()
         if step == 0:
-            halo_copies[0].wait_recv()
-            after = jnp.where(block == n_tm - 1, 0.0, halo[0])
-            here = series[...]
+            here, after = series[...], jnp.where(block == n_tm - 1, 0.0, halo[0])
         else:
-            halo_copies[step].wait_recv()
-            here = halo[step]
-            after = series[...] if step == 1 else halo[1]
+            here, after = halo[step], series[...] if step == 1 else halo[1]
         x = jnp.concatenate([here, after], axis=1)
-        xw[...] = x
-        mean, scale = window_stats(x)
-        mu[...] = mean[:, :rows]
-        sc[...] = scale[:, :rows]
-
-        acc[step] = jnp.zeros((rows, rows), jnp.float32)
-
-        def group(g, carry):
-            rows8 = pl.ds(pl.multiple_of(g * GROUP, GROUP), GROUP)
-            x8, mu8, sc8 = xw[rows8, :], mu[rows8, :], sc[rows8, :]
-            for r in range(GROUP):
-                def store(k, value, r=r):
-                    zbuf[r * WIN + k:r * WIN + k + 16, :] = value
-                build_channel(r, x8, mu8, sc8, store)
-            if step == 0:
-                zown[g] = zbuf[...].T
-            acc[step] += jnp.dot(zown[g], zbuf[...], preferred_element_type=jnp.float32)
-            return carry
-
-        lax.fori_loop(0, depth // GROUP, group, 0)
-
+        xt[0:reach, :] = jnp.concatenate([x[:, :reach], x[:, half:half + reach]], axis=0).T
+        span, source = 1, None
+        while span < half:
+            count = min(reach, -(-(reach - 2 * span) // 8) * 8)
+            target = 0 if source is None else 1 - source
+            mean_ref = xt if source is None else moments.at[source, 0]
+            mean, later = mean_ref[0:count, :], mean_ref[span:span + count, :]
+            gap = later - mean
+            second = gap * gap * (span * 0.5)
+            if source is not None:
+                second = second + (moments[source, 1, 0:count, :] + moments[source, 1, span:span + count, :])
+            moments[target, 0, 0:count, :] = (mean + later) * 0.5
+            moments[target, 1, 0:count, :] = second
+            span, source = 2 * span, target
+        mean, second = moments[source, 0, 0:rows, :], moments[source, 1, 0:rows, :]
+        later = pltpu.roll(mean, depth, 1)
+        gap = later - mean
+        second = second + pltpu.roll(second, depth, 1) + gap * gap * (half * 0.5)
+        mu[...] = (mean + later) * 0.5
+        sc[...] = lax.rsqrt(second * (1.0 / WIN) + EPS)
+
+    def build(step, g):
+        for tile in range(0, rows, 16):
+            m, s = mu[tile:tile + 16, :], sc[tile:tile + 16, :]
+            for k in range(GROUP):
+                z = (xt[pl.ds(g * GROUP + (tile + k), 16), :] - m) * s
+                windows[step][g, tile:tile + 16, 2 * depth * k:2 * depth * (k + 1)] = z.astype(jnp.bfloat16)
+
+    def multiply(step, g):
+        acc[step] += lax.dot_general(z0[g], windows[step][g], (((1,), (1,)), ((), ())),
+                                     preferred_element_type=jnp.float32)
+
+    def send(step):
         copies = []
         for d in range(1, n_chan):
             copy = pltpu.make_async_remote_copy(
@@ -112,7 +100,24 @@
             copies.append(copy)
         return copies
 
-    sent = [stage(step) for step in range(STEPS + 1)]
+    acc[...] = jnp.zeros_like(acc)
+    xt[reach:, :] = jnp.zeros((xt.shape[0] - reach, xt.shape[1]), jnp.float32)
+    moments[:, :, reach:, :] = jnp.zeros((2, 2, xt.shape[0] - reach, xt.shape[1]), jnp.float32)
+    sent = []
+    for step in range(STEPS + 2):
+        if step <= STEPS:
+            prepare(step)
+
+        def chunk(g, carry, step=step):
+            if step > 0:
+                multiply(step - 1, g)
+            if step <= STEPS:
+                build(step, g)
+            return carry
+
+        lax.fori_loop(0, chunks, chunk, 0)
+        if step > 0:
+            sent.append(send(step - 1))
 
     seg_len = rows // 2
     row_at = part * own + lax.broadcasted_iota(jnp.int32, (own, rows), 0)
@@ -178,11 +183,13 @@
             out_specs=vmem,
             scratch_shapes=[
                 pltpu.VMEM((STEPS + 1, depth, rows), jnp.float32),
-                pltpu.VMEM((depth, 2 * rows), jnp.float32),
-                pltpu.VMEM((depth, rows), jnp.float32),
-                pltpu.VMEM((depth, rows), jnp.float32),
-                pltpu.VMEM((depth // GROUP, rows, GROUP * WIN), jnp.bfloat16),
-                pltpu.VMEM((GROUP * WIN, rows), jnp.bfloat16),
+                pltpu.VMEM((rows + WIN // 2 + 16, 2 * depth), jnp.float32),
+                pltpu.VMEM((2, 2, rows + WIN // 2 + 16, 2 * depth), jnp.float32),
+                pltpu.VMEM((rows, 2 * depth), jnp.float32),
+                pltpu.VMEM((rows, 2 * depth), jnp.float32),
+                pltpu.VMEM((WIN // 2 // GROUP, rows, GROUP * 2 * depth), jnp.bfloat16),
+                pltpu.VMEM((WIN // 2 // GROUP, rows, GROUP * 2 * depth), jnp.bfloat16),
+                pltpu.VMEM((WIN // 2 // GROUP, rows, GROUP * 2 * depth), jnp.bfloat16),
                 pltpu.VMEM((STEPS + 1, rows, rows), jnp.float32),
                 pltpu.VMEM((STEPS + 1, n_chan - 1, own, rows), jnp.float32),
                 pltpu.VMEM((n_chan, 8, 128), jnp.float32),

time: 50.5 us -> 35.8 us (0.71); the launches traced: 49.8 us -> 35.6 us
  Pallas kernels: 48.5 us -> 34.4 us
    pallas_call x1, Pallas kernels: 48.5 us -> 34.4 us  [body(): pl.pallas_call(functools.partial(kernel, n_tm, n_chan), out_shape=jax.Sha...]
where the time goes in v2:
time: 35.8 us; the launch traced here: 35.6 us
  Pallas kernels  34.4 us (96%)
  local copies, waits for them, and re-layouts  1.22 us (3%)
    pallas_call x1, Pallas kernels, body(): pl.pallas_call(functools.partial(kernel, n_tm, n_chan), out_shape=jax.Sha...  34.4 us
    unnamed x3, local copies, waits for them, and re-layouts  1.22 us

profile of v2, /device:TPU:0, one launch (start us, length us, event | category | flops | bytes accessed | tf_op | source)
XLA Modules:
  0.0 35.6 jit_solution(842464393819819783)
XLA Ops:
  0.0 34.4 %shard_map.28 = f32[1,256]{1,0:T(1,128)} custom-call(s32[16]{0:T(128)} %lengths.1, f32[64,256]{1,0:T(8,128)} %series.1), custom_call_target="tpu_custom_call" | custom-call | tf_op jit(solution)/shard_map/pallas_call | solution.py:179
  34.4 0.0 copy-start
  34.4 0.7 %copy-done = f32[1,256]{1,0:T(1,128)S(1)} copy-done((f32[1,256]{1,0:T(1,128)S(1)}, f32[1,256]{1,0:T(1,128)}, u32[]{:S(2)}) %copy-start) | copy-done | bytes 1048
  35.1 0.6 %copy.4 = f32[256]{0:T(256)} copy(f32[256]{0:T(256)S(1)} %bitcast.1) | data formatting | bytes 2048
Async XLA Ops:
  34.4 0.7 %copy-start = (f32[1,256]{1,0:T(1,128)S(1)}, f32[1,256]{1,0:T(1,128)}, u32[]{:S(2)}) copy-start(f32[1,256]{1,0:T(1,128)} %shard_map.28) | copy-start | bytes 3076
